TPU v7x, 32 devices: a whole 2x2x4 slice. The times are simulated.
32 devices in a mesh: ctx: 8 (over z, core), tp: 4 (over y, x).
Axes of the slice: x: 2, y: 2, z: 4, core: 2. Of those that a mesh axis runs over, the one named last changes fastest.
Arguments:
- act_codes: bfloat16 [2048, 4096], P(('ctx', 'tp')), may hold values from -6 to 6
- scale_exps: int32 [2048, 32], P(('ctx', 'tp')), may hold values from -2 to 2
- weight: bfloat16 [4096, 6144], P(None, 'tp'), may hold values from -0.09375 to 0.09375
- grad_out: bfloat16 [2048, 6144], P('ctx', 'tp'), may hold values from -6 to 6
Outputs:
- grad_input: bfloat16 [2048, 4096], P(('ctx', 'tp'))
- grad_weight: float32 [4096, 6144], P('ctx', 'tp')
All inputs are finite; a program needn't handle non-finite values.
Results may differ from a plain program's by a relative error of at most 0.023.
Values may be sent and summed in bfloat16 or wider, within the bound.
A program may use at most 64 MiB of HBM per device.

v0:
```python
import jax
import jax.numpy as jnp
from jax import lax
from jax.sharding import PartitionSpec as P


def dequantize(codes, exponents, block):
    tok_rows, width = codes.shape
    scales = jnp.exp2(exponents.astype(jnp.float32))
    blocked = (
        codes.astype(jnp.float32).reshape(tok_rows, width // block, block) * scales[:, :, None]
    )
    return blocked.reshape(tok_rows, width).astype(jnp.bfloat16)


def body(act_codes, scale_exps, weight, grad_out):
    width = act_codes.shape[1]
    block = width // scale_exps.shape[1]
    acts = dequantize(act_codes, scale_exps, block)
    add_acts = lax.all_gather(acts, "tp", axis=0, tiled=True)
    grads = grad_out
    partial_sum = lax.dot_general(
        add_acts, grads, (((0,), (0,)), ((), ())), preferred_element_type=jnp.float32
    )
    summed = lax.psum_scatter(
        partial_sum.astype(jnp.bfloat16), "ctx", scatter_dimension=0, tiled=True
    ).astype(jnp.float32)
    tokens_all = grad_out.shape[0] * lax.axis_size("ctx")
    grad_weight = summed * lax.rsqrt(jnp.float32(tokens_all))
    grads = grad_out
    grad_input = lax.psum_scatter(
        lax.dot_general(
            grads, weight, (((1,), (1,)), ((), ())), preferred_element_type=jnp.float32
        ).astype(jnp.bfloat16),
        "tp",
        scatter_dimension=0,
        tiled=True,
    )
    return (grad_input, grad_weight)


def solution(mesh):
    placed = (P(("ctx", "tp"), None), P(("ctx", "tp"), None), P(None, "tp"), P("ctx", "tp"))
    return jax.shard_map(
        body,
        mesh=mesh,
        in_specs=placed,
        out_specs=(P(("ctx", "tp"), None), P("ctx", "tp")),
        check_vma=False,
    )
```

profile of v0, /device:TPU:0, one launch (start us, length us, event | category | flops | bytes accessed | tf_op | source)
XLA Modules:
  0.0 230.3 jit_solution(15797501050247371986)
XLA Ops:
  7.2 0.0 copy-start
  7.2 0.0 all-gather.2.cloned.1.call-start
  7.2 0.8 multiply_exponential_fusion
  8.0 0.1 copy.6
  8.1 0.3 mul.17
  8.4 2.4 %fusion = bf16[64,4096]{1,0:T(8,128)(2,1)} fusion(f32[8,8,32,128]{3,2,1,0:T(8,128)S(1)} %bitcast.9, bf16[64,4096]{1,0:T(8,128)(2,1)} %param.4), kind=kLoop, calls=%fused_computation.4 | loop fusion | flops 786432 | bytes 2097152 | tf_op jit(solution)/shard_map/convert_element_type | solution.py:13
  10.9 0.0 all-gather.2.cloned.1.call-update
  10.9 0.0 reduce-scatter.5.cloned.1.call-start
  10.9 38.0 %all-gather.2.cloned.1.call-done = bf16[256,4096]{1,0:T(8,128)(2,1)} async-done(((bf16[64,4096]{1,0:T(8,128)(2,1)}), bf16[256,4096]{1,0:T(8,128)(2,1)}) %all-gather.2.cloned.1.call-update) | async-done | bytes 2097168 | tf_op jit(solution)/shard_map/all_gather | solution.py:20
  49.0 0.0 copy-done
  49.0 8.3 %convolution_convert_fusion = bf16[4096,1536]{1,0:T(8,128)(2,1)} fusion(bf16[256,4096]{1,0:T(8,128)(2,1)} %all-gather.2.cloned.1.call-done, bf16[256,1536]{1,0:T(8,128)(2,1)S(1)} %copy-done), kind=kOutput, calls=%fused_computation | convolution fusion | flops 3227516928 | bytes 15466496 | tf_op jit(solution)/shard_map/dot_general | solution.py:22
  57.2 0.0 reduce-scatter.5.cloned.1.call-update
  57.3 0.0 reduce-scatter.3.cloned.1.call-start
  57.3 13.9 %convolution_convert_fusion.1 = bf16[256,4096]{1,0:T(8,128)(2,1)} fusion(bf16[256,1536]{1,0:T(8,128)(2,1)S(1)} %copy-done, bf16[4096,1536]{1,0:T(8,128)(2,1)} %param.6), kind=kOutput, calls=%fused_computation.1 | convolution fusion | flops 3222274048 | bytes 15466496 | tf_op jit(solution)/shard_map/dot_general | solution.py:32
  71.2 0.0 reduce-scatter.3.cloned.1.call-update
  71.2 115.3 %reduce-scatter.5.cloned.1.call-done = bf16[512,1536]{1,0:T(8,128)(2,1)} async-done(((bf16[4096,1536]{1,0:T(8,128)(2,1)}), bf16[512,1536]{1,0:T(8,128)(2,1)}) %reduce-scatter.5.cloned.1.call-update) | async-done | bytes 1572880 | tf_op jit(solution)/shard_map/reduce_scatter | solution.py:25
  186.6 3.5 %convert_multiply_fusion = f32[512,1536]{1,0:T(8,128)} fusion(bf16[512,1536]{1,0:T(8,128)(2,1)} %reduce-scatter.5.cloned.1.call-done), kind=kLoop, calls=%fused_computation.2 | loop fusion | flops 1572864 | bytes 4718592 | tf_op jit(solution)/shard_map/mul | solution.py:29
  190.1 33.7 %reduce-scatter.3.cloned.1.call-done = bf16[64,4096]{1,0:T(8,128)(2,1)} async-done(((bf16[256,4096]{1,0:T(8,128)(2,1)}), bf16[64,4096]{1,0:T(8,128)(2,1)}) %reduce-scatter.3.cloned.1.call-update) | async-done | bytes 524304 | tf_op jit(solution)/shard_map/reduce_scatter | solution.py:31
Async XLA Ops:
  7.2 41.8 %copy-start = (bf16[256,1536]{1,0:T(8,128)(2,1)S(1)}, bf16[256,1536]{1,0:T(8,128)(2,1)}, u32[]{:S(2)}) copy-start(bf16[256,1536]{1,0:T(8,128)(2,1)} %param.7) | copy-start | bytes 2359300
  7.2 41.8 %all-gather.2.cloned.1.call-start = ((), (), s32[]{:S(2)}) async-start(), calls=%async_computation.3 | async-start | bytes 2621440 | tf_op jit(solution)/shard_map/all_gather | solution.py:20
  10.9 175.7 %reduce-scatter.5.cloned.1.call-start = ((), (), s32[]{:S(2)}) async-start(), calls=%async_computation.4 | async-start | bytes 14155776 | tf_op jit(solution)/shard_map/reduce_scatter | solution.py:25
  57.3 166.5 %reduce-scatter.3.cloned.1.call-start = ((), (), s32[]{:S(2)}) async-start(), calls=%async_computation.2 | async-start | bytes 2621440 | tf_op jit(solution)/shard_map/reduce_scatter | solution.py:31
Sparse Core Ops, SparseCore 0:
  11.0 37.8 all-gather.1
  57.4 129.1 reduce-scatter.4
  190.1 33.6 reduce-scatter.2
where the time goes:
time: 231 us; the launch traced here: 230 us
  waiting for transfers between devices  187 us (81%)
  matrix products  22.2 us (10%)
  between operations  13.8 us (6%)
  other arithmetic  6.73 us (3%)
    reduce_scatter x1, waiting for transfers between devices, body(): lax.psum_scatter(partial_sum.astype(jnp.bfloat16), 'ctx', scatter_dimensi...  115 us
    all_gather x1, waiting for transfers between devices, body(): add_acts = lax.all_gather(acts, 'tp', axis=0, tiled=True)  38 us
    reduce_scatter x1, waiting for transfers between devices, body(): lax.psum_scatter(lax.dot_general(grads, weight, (((1,), (1,)), ((), ())),...  33.7 us
    dot_general x1, matrix products, body(): lax.dot_general(grads, weight, (((1,), (1,)), ((), ())), preferred_elemen...  13.9 us
    dot_general x1, matrix products, body(): lax.dot_general(add_acts, grads, (((0,), (0,)), ((), ())), preferred_elem...  8.29 us
  transfers between devices with their start and end apart: 3, of which 3 were waited for; matrix products, arithmetic and copies ran while one was open for 8% of the time, Pallas kernels for 0%

commit v1 on v0

v1 whole, which is shorter than its diff:
```python
import functools

import jax
import jax.numpy as jnp
from jax import lax
from jax.experimental import pallas as pl
from jax.experimental.pallas import tpu as pltpu
from jax.sharding import PartitionSpec as P

MESH = pl.DeviceIdType.MESH
CHUNKS = 2


def kernel(
    n_ctx, n_tp, tokens,
    codes_ref, exps_ref, weight_ref, grads_ref,
    gin_ref, gw_ref,
    w_buf, g_buf, a_send, a_buf, part, landed,
    w_sem, g_sem,
    a_ssem, a_rsem, b_ssem, b_rsem, up_ssem, down_ssem, mate_ssem, g_rsem, p_ssem, p_rsem,
):
    n_line = n_ctx // 2
    me = lax.axis_index("ctx")
    tp = lax.axis_index("tp")
    core = lax.rem(me, 2)
    z = lax.div(me, 2)
    mate = me + 1 - 2 * core
    rows, width = codes_ref.shape
    block = width // exps_ref.shape[1]
    feats = width // n_ctx
    d_tile = w_buf.shape[1]
    n_d = w_buf.shape[0]
    scale = lax.rsqrt(jnp.float32(tokens))
    split = n_ctx * n_tp <= 64

    def load_w(i):
        return pltpu.make_async_copy(
            weight_ref.at[pl.ds(i * d_tile, d_tile)], w_buf.at[i], w_sem.at[i]
        )

    def load_g(k):
        size = g_buf.shape[2]
        return pltpu.make_async_copy(
            grads_ref.at[pl.ds(k * size, size)], g_buf.at[me, k], g_sem.at[k]
        )

    for k in range(CHUNKS):
        load_g(k).start()
    for i in range(n_d):
        load_w(i).start()

    barrier = pltpu.get_barrier_semaphore()
    for r in range(1, n_ctx):
        pl.semaphore_signal(
            barrier, inc=1, device_id=(lax.rem(me + r, n_ctx), tp), device_id_type=MESH
        )
    for r in range(1, n_tp):
        pl.semaphore_signal(
            barrier, inc=1, device_id=(me, lax.rem(tp + r, n_tp)), device_id_type=MESH
        )

    for b in range(width // block):
        owner, place = divmod(b * block, feats)
        power = jnp.exp2(exps_ref[:, b : b + 1].astype(jnp.float32))
        value = codes_ref[:, b * block : (b + 1) * block].astype(jnp.float32) * power
        a_send[owner, :, place : place + block] = value.astype(jnp.bfloat16)

    pl.semaphore_wait(barrier, n_ctx + n_tp - 2)

    def remote(src, dst, ssem, rsem, to):
        return pltpu.make_async_remote_copy(
            src_ref=src, dst_ref=dst, send_sem=ssem, recv_sem=rsem,
            device_id=to, device_id_type=MESH,
        )

    def act_copy(to):
        return remote(
            a_send.at[to], a_buf.at[me, tp], a_ssem.at[to], a_rsem.at[me], (to, tp)
        )

    def act_landing(source):
        return remote(
            a_send.at[source], a_buf.at[source, tp], a_ssem.at[source], a_rsem.at[source],
            (source, tp),
        )

    def spread_copy(s, q, src=None):
        return remote(
            a_buf.at[s, tp] if src is None else src,
            a_buf.at[s, tp], b_ssem.at[s, q], b_rsem.at[s, tp], (me, q),
        )

    def spread_landing(s, q):
        return remote(
            a_buf.at[s, q], a_buf.at[s, q], b_ssem.at[s, q], b_rsem.at[s, q], (me, q)
        )

    def spread_all(q):
        return remote(
            a_buf.at[:, tp], a_buf.at[:, tp], b_ssem.at[0, q], b_rsem.at[0, tp], (me, q)
        )

    def spread_all_landing(q):
        return remote(
            a_buf.at[:, q], a_buf.at[:, q], b_ssem.at[0, q], b_rsem.at[0, q], (me, q)
        )

    def pass_on(s, k, ssem, to):
        return remote(
            g_buf.at[s, k], g_buf.at[s, k], ssem.at[lax.div(s, 2), k], g_rsem.at[s, k], (to, tp)
        )

    def up(s, k):
        return pass_on(s, k, up_ssem, me + 2)

    def down(s, k):
        return pass_on(s, k, down_ssem, me - 2)

    def across(s, k):
        return pass_on(s, k, mate_ssem, mate)

    has_up = z < n_line - 1
    has_down = z > 0

    for r in range(1, n_ctx):
        act_copy(lax.rem(me + r, n_ctx)).start()
    for k in range(CHUNKS):
        load_g(k).wait()

        @pl.when(has_up)
        def _():
            up(me, k).start()

        @pl.when(has_down)
        def _():
            down(me, k).start()

        across(me, k).start()

    peers = [lax.rem(tp + r, n_tp) for r in range(1, n_tp)]
    if split:
        for q in peers:
            spread_copy(me, q, a_send.at[me]).start()
    a_buf[me, tp] = a_send[me]
    for r in range(1, n_ctx):
        s = lax.rem(me + r, n_ctx)
        act_landing(s).wait_recv()
        if split:
            for q in peers:
                spread_copy(s, q).start()
    if not split:
        for q in peers:
            spread_all(q).start()

    grads = g_buf[me].reshape(-1, g_buf.shape[3])
    for i in range(n_d):
        load_w(i).wait()
        piece = lax.dot_general(
            grads, w_buf[i], (((1,), (1,)), ((), ())), preferred_element_type=jnp.float32
        ).astype(jnp.bfloat16)
        part[:, :, i * d_tile : (i + 1) * d_tile] = piece.reshape(n_tp, rows, d_tile)

    def part_copy(q):
        return remote(part.at[q], landed.at[tp], p_ssem.at[q], p_rsem.at[tp], (me, q))

    def part_landing(q):
        return remote(part.at[q], landed.at[q], p_ssem.at[q], p_rsem.at[q], (me, q))

    for q in peers:
        part_copy(q).start()

    n_cols = g_buf.shape[3]
    n_tile = 512 if n_cols % 512 == 0 else n_cols

    def accumulate(zz, first):
        lhs = a_buf[pl.ds(2 * zz, 2)].reshape(-1, feats).T

        for j in range(n_cols // n_tile):
            cols = slice(j * n_tile, (j + 1) * n_tile)
            rhs = g_buf[pl.ds(2 * zz, 2), :, :, cols].reshape(-1, n_tile)
            term = jnp.dot(lhs, rhs, preferred_element_type=jnp.float32) * scale
            if first:
                gw_ref[:, cols] = term
            else:
                gw_ref[:, cols] += term

    def chip_terms(zz, first=False):
        other = 2 * zz + 1 - core
        for k in range(CHUNKS):
            across(other, k).wait_recv()
        if split:
            for c in range(2):
                for q in peers:
                    spread_landing(2 * zz + c, q).wait_recv()
        elif first:
            for q in peers:
                spread_all_landing(q).wait_recv()
        accumulate(zz, first)

    def terms_at(d):
        if d == 0:
            chip_terms(z, True)
            return

        @pl.when(z >= d)
        def _():
            chip_terms(z - d)

        @pl.when(z + d < n_line)
        def _():
            chip_terms(z + d)

    def sum_parts():
        for q in peers:
            part_landing(q).wait_recv()
        total = part[tp].astype(jnp.float32)
        for q in peers:
            total = total + landed[q].astype(jnp.float32)
        gin_ref[...] = total.astype(jnp.bfloat16)

    for d in range(1, n_line):
        if d == n_line - 1:
            sum_parts()
        for k in range(CHUNKS):

            @pl.when(z >= d)
            def _():
                s = me - 2 * d
                up(s, k).wait_recv()

                @pl.when(has_up)
                def _():
                    up(s, k).start()

                across(s, k).start()

            @pl.when(z + d < n_line)
            def _():
                s = me + 2 * d
                down(s, k).wait_recv()

                @pl.when(has_down)
                def _():
                    down(s, k).start()

                across(s, k).start()

        terms_at(d - 1)
    terms_at(n_line - 1)

    for r in range(1, n_ctx):
        act_copy(lax.rem(me + r, n_ctx)).wait_send()
    for q in peers:
        part_copy(q).wait_send()
        if split:
            for s in range(n_ctx):
                spread_copy(s, q).wait_send()
        else:
            spread_all(q).wait_send()
    for zz in range(n_line):
        for k in range(CHUNKS):
            s = 2 * zz + core
            across(s, k).wait_send()

            @pl.when(has_up & (zz <= z))
            def _():
                up(s, k).wait_send()

            @pl.when(has_down & (zz >= z))
            def _():
                down(s, k).wait_send()


def body(act_codes, scale_exps, weight, grad_out):
    n_ctx, n_tp = lax.axis_size("ctx"), lax.axis_size("tp")
    n_line = n_ctx // 2
    rows, width = act_codes.shape
    toks, cols = grad_out.shape
    feats = width // n_ctx
    d_tile = min(512, width)
    dma = pltpu.SemaphoreType.DMA
    vmem = pl.BlockSpec(memory_space=pltpu.VMEM)
    hbm = pl.BlockSpec(memory_space=pl.ANY)
    bf16 = jnp.bfloat16
    return pl.pallas_call(
        functools.partial(kernel, n_ctx, n_tp, toks * n_ctx),
        out_shape=(
            jax.ShapeDtypeStruct((rows, width), bf16),
            jax.ShapeDtypeStruct((feats, cols), jnp.float32),
        ),
        in_specs=[vmem, vmem, hbm, hbm],
        out_specs=(vmem, vmem),
        scratch_shapes=[
            pltpu.VMEM((width // d_tile, d_tile, cols), bf16),
            pltpu.VMEM((n_ctx, CHUNKS, toks // CHUNKS, cols), bf16),
            pltpu.VMEM((n_ctx, rows, feats), bf16),
            pltpu.VMEM((n_ctx, n_tp, rows, feats), bf16),
            pltpu.VMEM((n_tp, rows, width), bf16),
            pltpu.VMEM((n_tp, rows, width), bf16),
            dma((width // d_tile,)),
            dma((CHUNKS,)),
            dma((n_ctx,)),
            dma((n_ctx,)),
            dma((n_ctx if n_ctx * n_tp <= 64 else 1, n_tp)),
            dma((n_ctx if n_ctx * n_tp <= 64 else 1, n_tp)),
            dma((n_line, CHUNKS)),
            dma((n_line, CHUNKS)),
            dma((n_line, CHUNKS)),
            dma((n_ctx, CHUNKS)),
            dma((n_tp,)),
            dma((n_tp,)),
        ],
        compiler_params=pltpu.CompilerParams(
            collective_id=0, has_side_effects=True, vmem_limit_bytes=60 * 1024 * 1024
        ),
    )(act_codes, scale_exps, weight, grad_out)


def solution(mesh):
    placed = (P(("ctx", "tp"), None), P(("ctx", "tp"), None), P(None, "tp"), P("ctx", "tp"))
    return jax.shard_map(
        body,
        mesh=mesh,
        in_specs=placed,
        out_specs=(P(("ctx", "tp"), None), P("ctx", "tp")),
        check_vma=False,
    )
```

time: 231 us -> 79.8 us (0.35)
  waiting for transfers between devices: 187 us -> 0 us
  Pallas kernels: 0 us -> 71.8 us
  matrix products: 22.2 us -> 0 us
  between operations: 13.8 us -> 0.64 us
  other arithmetic: 6.73 us -> 0 us
  local copies, waits for them, and re-layouts: 0.43 us -> 7.04 us
    reduce_scatter x2 -> x0, waiting for transfers between devices: 149 us -> none  [the longest x1 115 us: body(): lax.psum_scatter(partial_sum.astype(jnp.bfloat16), 'ctx', scatter_dimensi...]
    pallas_call x0 -> x1, Pallas kernels: none -> 71.8 us  [body(): pl.pallas_call(functools.partial(kernel, n_ctx, n_tp, toks * n_ctx), out_...]
    all_gather x1 -> x0, waiting for transfers between devices: 38 us -> none  [body(): add_acts = lax.all_gather(acts, 'tp', axis=0, tiled=True)]
    dot_general x2 -> x0, matrix products: 22.2 us -> none  [the longest x1 13.9 us: body(): lax.dot_general(grads, weight, (((1,), (1,)), ((), ())), preferred_elemen...]
    unnamed x2 -> x3, local copies, waits for them, and re-layouts: 0.01 us -> 7.04 us
    mul x1 -> x0, other arithmetic: 3.51 us -> none  [body(): grad_weight = summed * lax.rsqrt(jnp.float32(tokens_all))]
    convert_element_type x1 -> x0, other arithmetic: 2.44 us -> none  [dequantize(): return blocked.reshape(tok_rows, width).astype(jnp.bfloat16)]
  transfers between devices with their start and end apart: 3 -> 0, of which waited for: 3 -> 0; matrix products, arithmetic and copies ran while one was open for 8% -> 0% of each run, Pallas kernels for 0% -> 0%
where the time goes in v1:
time: 79.8 us; the launch traced here: 79.5 us
  Pallas kernels  71.8 us (90%)
  local copies, waits for them, and re-layouts  7.04 us (9%)
    pallas_call x1, Pallas kernels, body(): pl.pallas_call(functools.partial(kernel, n_ctx, n_tp, toks * n_ctx), out_...  71.8 us
    unnamed x3, local copies, waits for them, and re-layouts  7.04 us

profile of v1, /device:TPU:0, one launch (start us, length us, event | category | flops | bytes accessed | tf_op | source)
XLA Modules:
  0.0 79.5 jit_solution(15365599037272941119)
XLA Ops:
  0.6 1.4 %copy.6.exps_ref = s32[64,32]{1,0:T(8,128)} copy(s32[64,32]{0,1:T(8,128)} %param.5) | data formatting | bytes 16384 | tf_op args[1]
  2.0 71.8 %shard_map.59 = (bf16[64,4096]{1,0:T(8,128)(2,1)}, f32[512,1536]{1,0:T(8,128)}) custom-call(bf16[64,4096]{1,0:T(8,128)(2,1)} %codes_ref.1, s32[64,32]{1,0:T(8,128)} %copy.6.exps_ref, bf16[4096,1536]{1,0:T(8,128)(2,1)} %weight_ref.1, bf16[256,1536]{1,0:T(8,128)(2,1)} %grads_ref.1), custom_call_target="tpu_custom_call" | custom-call | tf_op jit(solution)/shard_map/pallas_call | solution.py:285
  73.9 1.9 %copy.9 = bf16[64,4096]{1,0:T(8,128)(2,1)} copy(bf16[64,4096]{1,0:T(8,128)(2,1)} %get-tuple-element.4) | data formatting | bytes 1048576
  75.8 3.8 %copy.10 = f32[512,1536]{1,0:T(8,128)} copy(f32[512,1536]{1,0:T(8,128)} %get-tuple-element.5) | data formatting | bytes 6291456

commit v2 on v1

--- a/solution.py
+++ b/solution.py
@@ -8,15 +8,15 @@
 from jax.sharding import PartitionSpec as P
 
 MESH = pl.DeviceIdType.MESH
-CHUNKS = 2
+CHUNKS = 4
 
 
 def kernel(
     n_ctx, n_tp, tokens,
-    codes_ref, exps_ref, weight_ref, grads_ref,
+    codes_hbm, exps_hbm, weight_ref, grads_ref,
     gin_ref, gw_ref,
-    w_buf, g_buf, a_send, a_buf, part, landed,
-    w_sem, g_sem,
+    codes_ref, exps_ref, w_buf, g_buf, a_send, a_buf, part, landed,
+    in_sem, w_sem, g_sem,
     a_ssem, a_rsem, b_ssem, b_rsem, up_ssem, down_ssem, mate_ssem, g_rsem, p_ssem, p_rsem,
 ):
     n_line = n_ctx // 2
@@ -26,7 +26,7 @@
     z = lax.div(me, 2)
     mate = me + 1 - 2 * core
     rows, width = codes_ref.shape
-    block = width // exps_ref.shape[1]
+    block = width // exps_ref.shape[0]
     feats = width // n_ctx
     d_tile = w_buf.shape[1]
     n_d = w_buf.shape[0]
@@ -44,7 +44,12 @@
             grads_ref.at[pl.ds(k * size, size)], g_buf.at[me, k], g_sem.at[k]
         )
 
-    for k in range(CHUNKS):
+    load_codes = pltpu.make_async_copy(codes_hbm, codes_ref, in_sem.at[0])
+    load_exps = pltpu.make_async_copy(exps_hbm, exps_ref, in_sem.at[1])
+    load_g(0).start()
+    load_codes.start()
+    load_exps.start()
+    for k in range(1, CHUNKS):
         load_g(k).start()
     for i in range(n_d):
         load_w(i).start()
@@ -59,12 +64,6 @@
             barrier, inc=1, device_id=(me, lax.rem(tp + r, n_tp)), device_id_type=MESH
         )
 
-    for b in range(width // block):
-        owner, place = divmod(b * block, feats)
-        power = jnp.exp2(exps_ref[:, b : b + 1].astype(jnp.float32))
-        value = codes_ref[:, b * block : (b + 1) * block].astype(jnp.float32) * power
-        a_send[owner, :, place : place + block] = value.astype(jnp.bfloat16)
-
     pl.semaphore_wait(barrier, n_ctx + n_tp - 2)
 
     def remote(src, dst, ssem, rsem, to):
@@ -122,26 +121,38 @@
     has_up = z < n_line - 1
     has_down = z > 0
 
+    def send_own(k):
+        load_g(k).wait()
+
+        @pl.when(has_up)
+        def _():
+            up(me, k).start()
+
+        @pl.when(has_down)
+        def _():
+            down(me, k).start()
+
+        across(me, k).start()
+
+    send_own(0)
+    load_codes.wait()
+    load_exps.wait()
+    powers = jnp.exp2(exps_ref[...].astype(jnp.float32)).T
+    for b in range(width // block):
+        owner, place = divmod(b * block, feats)
+        value = codes_ref[:, b * block : (b + 1) * block].astype(jnp.float32)
+        value = value * powers[:, b : b + 1]
+        a_send[owner, :, place : place + block] = value.astype(jnp.bfloat16)
+    a_buf[me, tp] = a_send[me]
     for r in range(1, n_ctx):
         act_copy(lax.rem(me + r, n_ctx)).start()
-    for k in range(CHUNKS):
-        load_g(k).wait()
-
-        @pl.when(has_up)
-        def _():
-            up(me, k).start()
-
-        @pl.when(has_down)
-        def _():
-            down(me, k).start()
-
-        across(me, k).start()
+    for k in range(1, CHUNKS):
+        send_own(k)
 
     peers = [lax.rem(tp + r, n_tp) for r in range(1, n_tp)]
     if split:
         for q in peers:
             spread_copy(me, q, a_send.at[me]).start()
-    a_buf[me, tp] = a_send[me]
     for r in range(1, n_ctx):
         s = lax.rem(me + r, n_ctx)
         act_landing(s).wait_recv()
@@ -172,22 +183,26 @@
     n_cols = g_buf.shape[3]
     n_tile = 512 if n_cols % 512 == 0 else n_cols
 
-    def accumulate(zz, first):
-        lhs = a_buf[pl.ds(2 * zz, 2)].reshape(-1, feats).T
+    def accumulate(zz, first, k=None):
+        if k is None:
+            lhs = a_buf[pl.ds(2 * zz, 2)].reshape(-1, feats).T
+        else:
+            size = n_tp // CHUNKS
+            lhs = a_buf[pl.ds(2 * zz, 2), k * size : (k + 1) * size].reshape(-1, feats).T
 
         for j in range(n_cols // n_tile):
             cols = slice(j * n_tile, (j + 1) * n_tile)
-            rhs = g_buf[pl.ds(2 * zz, 2), :, :, cols].reshape(-1, n_tile)
+            if k is None:
+                rhs = g_buf[pl.ds(2 * zz, 2), :, :, cols].reshape(-1, n_tile)
+            else:
+                rhs = g_buf[pl.ds(2 * zz, 2), k, :, cols].reshape(-1, n_tile)
             term = jnp.dot(lhs, rhs, preferred_element_type=jnp.float32) * scale
             if first:
                 gw_ref[:, cols] = term
             else:
                 gw_ref[:, cols] += term
 
-    def chip_terms(zz, first=False):
-        other = 2 * zz + 1 - core
-        for k in range(CHUNKS):
-            across(other, k).wait_recv()
+    def await_acts(zz, first):
         if split:
             for c in range(2):
                 for q in peers:
@@ -195,6 +210,12 @@
         elif first:
             for q in peers:
                 spread_all_landing(q).wait_recv()
+
+    def chip_terms(zz, first=False):
+        other = 2 * zz + 1 - core
+        for k in range(CHUNKS):
+            across(other, k).wait_recv()
+        await_acts(zz, first)
         accumulate(zz, first)
 
     def terms_at(d):
@@ -218,35 +239,66 @@
             total = total + landed[q].astype(jnp.float32)
         gin_ref[...] = total.astype(jnp.bfloat16)
 
-    for d in range(1, n_line):
-        if d == n_line - 1:
-            sum_parts()
+    def from_below(d, k):
+        s = me - 2 * d
+        up(s, k).wait_recv()
+
+        @pl.when(has_up)
+        def _():
+            up(s, k).start()
+
+        across(s, k).start()
+
+    def from_above(d, k):
+        s = me + 2 * d
+        down(s, k).wait_recv()
+
+        @pl.when(has_down)
+        def _():
+            down(s, k).start()
+
+        across(s, k).start()
+
+    for d in range(1, n_line - 1):
         for k in range(CHUNKS):
 
             @pl.when(z >= d)
             def _():
-                s = me - 2 * d
-                up(s, k).wait_recv()
-
-                @pl.when(has_up)
-                def _():
-                    up(s, k).start()
-
-                across(s, k).start()
+                from_below(d, k)
 
             @pl.when(z + d < n_line)
             def _():
-                s = me + 2 * d
-                down(s, k).wait_recv()
-
-                @pl.when(has_down)
-                def _():
-                    down(s, k).start()
-
-                across(s, k).start()
+                from_above(d, k)
 
         terms_at(d - 1)
-    terms_at(n_line - 1)
+
+    d = n_line - 1
+    terms_at(d - 1)
+
+    def last_terms(zz, arrive):
+        other = 2 * zz + 1 - core
+        await_acts(zz, False)
+        for k in range(CHUNKS):
+            arrive(d, k)
+            if k == CHUNKS - 1:
+                sum_parts()
+            if k > 0:
+                across(other, k - 1).wait_recv()
+                accumulate(zz, False, k - 1)
+        across(other, CHUNKS - 1).wait_recv()
+        accumulate(zz, False, CHUNKS - 1)
+
+    @pl.when(z == d)
+    def _():
+        last_terms(0, from_below)
+
+    @pl.when(z == 0)
+    def _():
+        last_terms(d, from_above)
+
+    @pl.when((z > 0) & (z < d))
+    def _():
+        sum_parts()
 
     for r in range(1, n_ctx):
         act_copy(lax.rem(me + r, n_ctx)).wait_send()
@@ -280,23 +332,26 @@
     d_tile = min(512, width)
     dma = pltpu.SemaphoreType.DMA
     vmem = pl.BlockSpec(memory_space=pltpu.VMEM)
-    hbm = pl.BlockSpec(memory_space=pl.ANY)
+    hbm = pl.BlockSpec(memory_space=pltpu.HBM)
     bf16 = jnp.bfloat16
     return pl.pallas_call(
         functools.partial(kernel, n_ctx, n_tp, toks * n_ctx),
         out_shape=(
-            jax.ShapeDtypeStruct((rows, width), bf16),
-            jax.ShapeDtypeStruct((feats, cols), jnp.float32),
+            pltpu.VMEM((rows, width), bf16),
+            pltpu.VMEM((feats, cols), jnp.float32),
         ),
-        in_specs=[vmem, vmem, hbm, hbm],
+        in_specs=[hbm, hbm, hbm, hbm],
         out_specs=(vmem, vmem),
         scratch_shapes=[
+            pltpu.VMEM((rows, width), bf16),
+            pltpu.VMEM(scale_exps.shape[::-1], scale_exps.dtype),
             pltpu.VMEM((width // d_tile, d_tile, cols), bf16),
             pltpu.VMEM((n_ctx, CHUNKS, toks // CHUNKS, cols), bf16),
             pltpu.VMEM((n_ctx, rows, feats), bf16),
             pltpu.VMEM((n_ctx, n_tp, rows, feats), bf16),
             pltpu.VMEM((n_tp, rows, width), bf16),
             pltpu.VMEM((n_tp, rows, width), bf16),
+            dma((2,)),
             dma((width // d_tile,)),
             dma((CHUNKS,)),
             dma((n_ctx,)),
@@ -311,9 +366,9 @@
             dma((n_tp,)),
         ],
         compiler_params=pltpu.CompilerParams(
-            collective_id=0, has_side_effects=True, vmem_limit_bytes=60 * 1024 * 1024
+            collective_id=0, has_side_effects=True, vmem_limit_bytes=40 * 1024 * 1024
         ),
-    )(act_codes, scale_exps, weight, grad_out)
+    )(act_codes, scale_exps.T, weight, grad_out)
 
 
 def solution(mesh):

time: 79.8 us -> 76 us (0.952)
  Pallas kernels: 71.8 us -> 69.8 us
  local copies, waits for them, and re-layouts: 7.04 us -> 5.34 us
    pallas_call x1, Pallas kernels: 71.8 us -> 69.8 us  [body(): pl.pallas_call(functools.partial(kernel, n_ctx, n_tp, toks * n_ctx), out_...]
    unnamed x3 -> x8, local copies, waits for them, and re-layouts: 7.04 us -> 5.34 us
where the time goes in v2:
time: 76 us; the launch traced here: 75.8 us
  Pallas kernels  69.8 us (92%)
  local copies, waits for them, and re-layouts  5.34 us (7%)
    pallas_call x1, Pallas kernels, body(): pl.pallas_call(functools.partial(kernel, n_ctx, n_tp, toks * n_ctx), out_...  69.8 us
    unnamed x8, local copies, waits for them, and re-layouts  5.34 us

profile of v2, /device:TPU:0, one launch (start us, length us, event | category | flops | bytes accessed | tf_op | source)
XLA Modules:
  0.0 75.8 jit_solution(15724138332584614514)
XLA Ops:
  0.6 0.0 copy-start
  0.6 1.1 %copy-done = bf16[256,1536]{1,0:T(8,128)(2,1)S(1)} copy-done((bf16[256,1536]{1,0:T(8,128)(2,1)S(1)}, bf16[256,1536]{1,0:T(8,128)(2,1)}, u32[]{:S(2)}) %copy-start) | copy-done | bytes 786456
  1.8 0.0 copy-start.1
  1.8 1.0 %copy-done.1 = bf16[64,4096]{1,0:T(8,128)(2,1)S(1)} copy-done((bf16[64,4096]{1,0:T(8,128)(2,1)S(1)}, bf16[64,4096]{1,0:T(8,128)(2,1)}, u32[]{:S(2)}) %copy-start.1) | copy-done | bytes 524312
  2.8 0.0 copy-start.2
  2.8 0.7 copy-done.2
  3.5 69.8 %shard_map.59 = (bf16[64,4096]{1,0:T(8,128)(2,1)S(1)}, f32[512,1536]{1,0:T(8,128)S(1)}) custom-call(bf16[64,4096]{1,0:T(8,128)(2,1)S(1)} %copy-done.1, s32[32,64]{1,0:T(8,128)S(1)} %bitcast.1, bf16[4096,1536]{1,0:T(8,128)(2,1)} %weight_ref.1, bf16[256,1536]{1,0:T(8,128)(2,1)S(1)} %copy-done), custom_call_target="tpu_custom_call" | custom-call | tf_op jit(solution)/shard_map/pallas_call | solution.py:337
  73.3 0.8 %copy.8 = bf16[64,4096]{1,0:T(8,128)(2,1)} copy(bf16[64,4096]{1,0:T(8,128)(2,1)S(1)} %get-tuple-element.2) | data formatting | bytes 1048576
  74.1 1.7 %copy.9 = f32[512,1536]{1,0:T(8,128)} copy(f32[512,1536]{1,0:T(8,128)S(1)} %get-tuple-element.3) | data formatting | bytes 6291456
Async XLA Ops:
  0.6 1.1 %copy-start = (bf16[256,1536]{1,0:T(8,128)(2,1)S(1)}, bf16[256,1536]{1,0:T(8,128)(2,1)}, u32[]{:S(2)}) copy-start(bf16[256,1536]{1,0:T(8,128)(2,1)} %grads_ref.1) | copy-start | bytes 2359300
  1.8 1.0 %copy-start.1 = (bf16[64,4096]{1,0:T(8,128)(2,1)S(1)}, bf16[64,4096]{1,0:T(8,128)(2,1)}, u32[]{:S(2)}) copy-start(bf16[64,4096]{1,0:T(8,128)(2,1)} %codes_hbm.1) | copy-start | bytes 1572868
  2.8 0.7 copy-start.2

commit v3 on v2

--- a/solution.py
+++ b/solution.py
@@ -153,23 +153,33 @@
     if split:
         for q in peers:
             spread_copy(me, q, a_send.at[me]).start()
+
+    grads = g_buf.at[me]
+
+    def part_piece(i):
+        load_w(i).wait()
+        rows_all = grads[...].reshape(-1, g_buf.shape[3])
+        piece = lax.dot_general(
+            rows_all, w_buf[i], (((1,), (1,)), ((), ())), preferred_element_type=jnp.float32
+        ).astype(jnp.bfloat16)
+        part[:, :, i * d_tile : (i + 1) * d_tile] = piece.reshape(n_tp, rows, d_tile)
+
+    per = -(-n_d // n_ctx)
+    done = 0
     for r in range(1, n_ctx):
-        s = lax.rem(me + r, n_ctx)
+        for i in range(done, min(done + per, n_d)):
+            part_piece(i)
+        done = min(done + per, n_d)
+        s = lax.rem(me - r + n_ctx, n_ctx)
         act_landing(s).wait_recv()
         if split:
             for q in peers:
                 spread_copy(s, q).start()
+    for i in range(done, n_d):
+        part_piece(i)
     if not split:
         for q in peers:
             spread_all(q).start()
-
-    grads = g_buf[me].reshape(-1, g_buf.shape[3])
-    for i in range(n_d):
-        load_w(i).wait()
-        piece = lax.dot_general(
-            grads, w_buf[i], (((1,), (1,)), ((), ())), preferred_element_type=jnp.float32
-        ).astype(jnp.bfloat16)
-        part[:, :, i * d_tile : (i + 1) * d_tile] = piece.reshape(n_tp, rows, d_tile)
 
     def part_copy(q):
         return remote(part.at[q], landed.at[tp], p_ssem.at[q], p_rsem.at[tp], (me, q))
@@ -331,6 +341,8 @@
     feats = width // n_ctx
     d_tile = min(512, width)
     dma = pltpu.SemaphoreType.DMA
+    lanes = -(-cols // 128) * 128
+    outs = -(-rows // 16) * 16 * width * 2 + feats * lanes * 4
     vmem = pl.BlockSpec(memory_space=pltpu.VMEM)
     hbm = pl.BlockSpec(memory_space=pltpu.HBM)
     bf16 = jnp.bfloat16
@@ -366,7 +378,7 @@
             dma((n_tp,)),
         ],
         compiler_params=pltpu.CompilerParams(
-            collective_id=0, has_side_effects=True, vmem_limit_bytes=40 * 1024 * 1024
+            collective_id=0, has_side_effects=True, vmem_limit_bytes=67_043_328 - outs - 8192
         ),
     )(act_codes, scale_exps.T, weight, grad_out)
 

time: 76 us -> 73 us (0.961)
  local copies, waits for them, and re-layouts: 5.34 us -> 2.46 us
    unnamed x8 -> x2, local copies, waits for them, and re-layouts: 5.34 us -> 2.46 us
where the time goes in v3:
time: 73 us; the launch traced here: 72.7 us
  Pallas kernels  69.6 us (95%)
  local copies, waits for them, and re-layouts  2.46 us (3%)
    pallas_call x1, Pallas kernels, body(): pl.pallas_call(functools.partial(kernel, n_ctx, n_tp, toks * n_ctx), out_...  69.6 us
    unnamed x2, local copies, waits for them, and re-layouts  2.46 us

profile of v3, /device:TPU:0, one launch (start us, length us, event | category | flops | bytes accessed | tf_op | source)
XLA Modules:
  0.0 72.7 jit_solution(14699198809055646251)
XLA Ops:
  0.6 69.6 %shard_map.59 = (bf16[64,4096]{1,0:T(8,128)(2,1)S(1)}, f32[512,1536]{1,0:T(8,128)S(1)}) custom-call(bf16[64,4096]{1,0:T(8,128)(2,1)} %codes_hbm.1, s32[32,64]{1,0:T(8,128)} %bitcast.1, bf16[4096,1536]{1,0:T(8,128)(2,1)} %weight_ref.1, bf16[256,1536]{1,0:T(8,128)(2,1)} %grads_ref.1), custom_call_target="tpu_custom_call" | custom-call | tf_op jit(solution)/shard_map/pallas_call | solution.py:349
  70.2 0.8 %copy.8 = bf16[64,4096]{1,0:T(8,128)(2,1)} copy(bf16[64,4096]{1,0:T(8,128)(2,1)S(1)} %get-tuple-element.2) | data formatting | bytes 1048576
  71.0 1.7 %copy.9 = f32[512,1536]{1,0:T(8,128)} copy(f32[512,1536]{1,0:T(8,128)S(1)} %get-tuple-element.3) | data formatting | bytes 6291456
